TPU v7x, 32 devices: a whole 2x2x4 slice. The times are simulated.
32 devices in a mesh: grp: 2 (over core), gx: 4 (over z), gy: 4 (over y, x).
Axes of the slice: x: 2, y: 2, z: 4, core: 2. Of those that a mesh axis runs over, the one named last changes fastest.
Arguments:
- coarse_ez: float32 [256, 1024], P('gx', ('grp', 'gy')), may hold values from -6 to 6
- coarse_hx: float32 [256, 1024], P('gx', ('grp', 'gy')), may hold values from -6 to 6
- coarse_hy: float32 [256, 1024], P('gx', ('grp', 'gy')), may hold values from -6 to 6
- coarse_ids: int32 [256, 1024], P('gx', ('grp', 'gy')), may hold values from 0 to 7
- mat_eps: float32 [8], replicated, may hold values from 1 to 12
- mat_sig: float32 [8], replicated, may hold values from 0 to 0.5
- fine_ez: float32 [4, 8, 32, 2304], P(None, ('grp', 'gy'), 'gx'), may hold values from -6 to 6
- fine_hx: float32 [4, 8, 32, 2304], P(None, ('grp', 'gy'), 'gx'), may hold values from -6 to 6
- fine_hy: float32 [4, 8, 32, 2304], P(None, ('grp', 'gy'), 'gx'), may hold values from -6 to 6
- fine_ids: int32 [4, 8, 32, 2304], P(None, ('grp', 'gy'), 'gx'), may hold values from 0 to 7
- boxes: int32 [4, 8, 32, 4], P('gx', ('grp', 'gy')), may hold values from 1 to 14, as said below
- src_cells: int32 [4], replicated, may hold values from 0 to 262143
- src_wave: float32 [3, 4], replicated, may hold values from -6 to 6
- rcv_cells: int32 [128], replicated, may hold values from 0 to 262143
Outputs:
- end_ez: float32 [256, 1024], P('gx', ('grp', 'gy'))
- end_hx: float32 [256, 1024], P('gx', ('grp', 'gy'))
- end_hy: float32 [256, 1024], P('gx', ('grp', 'gy'))
- end_fine_ez: float32 [4, 8, 32, 2304], P(None, ('grp', 'gy'), 'gx')
- end_fine_hx: float32 [4, 8, 32, 2304], P(None, ('grp', 'gy'), 'gx')
- end_fine_hy: float32 [4, 8, 32, 2304], P(None, ('grp', 'gy'), 'gx')
- traces: float32 [3, 128], replicated
Inputs may be any that keep to these rules, and one draw needn't show every extreme that they name: `boxes`: each box lies one cell or more inside its tile: corner + size <= 15; sizes are 4 to 14, drawn independently for every subgrid.
All inputs are finite; a program needn't handle non-finite values.
Results may differ from a plain program's by a relative error of at most 0.00011.
Values sent between devices are 32-bit elements; how exact they have to be, the bound alone decides.
No kernel may reach another device: no remote copies, remote signals or barrier semaphores. Data moves between devices by JAX's collectives and lax.ppermute only.
A program may use at most 64 MiB of HBM per device.

v0:
```python
import jax
import jax.numpy as jnp
from jax import lax
from jax.sharding import PartitionSpec as P

TILE = 16
STEPS = 3
COURANT = 0.5
HCOEF = 0.5


def passed_along(value, axis, steps):
    count = lax.axis_size(axis)
    initial, last = (max(0, -steps), min(count, count - steps))
    return lax.ppermute(value, axis, [(source, source + steps) for source in range(initial, last)])


def coefficients(ids, eps_table, sig_table, ratio):
    damp = jnp.zeros(ids.shape, jnp.float32)
    gain = jnp.zeros(ids.shape, jnp.float32)
    for material in range(eps_table.shape[0]):
        loss = sig_table[material] / (eps_table[material] * ratio)
        hit = ids == material
        damp = jnp.where(hit, (1.0 - loss) / (1.0 + loss), damp)
        gain = jnp.where(hit, COURANT / (eps_table[material] * (1.0 + loss)), gain)
    return (damp, gain)


def box_masks(boxes, cells, scale):
    coarse_of = jnp.arange(cells, dtype=jnp.int32) // scale
    low_i = boxes[..., 0:1]
    low_j = boxes[..., 1:2]
    high_i = low_i + boxes[..., 2:3]
    high_j = low_j + boxes[..., 3:4]
    rows_in = (coarse_of >= low_i) & (coarse_of < high_i)
    cols_in = (coarse_of >= low_j) & (coarse_of < high_j)
    rows_mid = (coarse_of > low_i) & (coarse_of < high_i - 1)
    cols_mid = (coarse_of > low_j) & (coarse_of < high_j - 1)
    inbox = rows_in[..., :, None] & cols_in[..., None, :]
    middle = rows_mid[..., :, None] & cols_mid[..., None, :]
    return (inbox, middle)


def flat_masks(boxes):
    width = TILE * 3
    index = jnp.arange(width * width, dtype=jnp.int32)
    coarse_i = index // width // 3
    coarse_j = index % width // 3
    low_i = boxes[:, 0:1]
    low_j = boxes[:, 1:2]
    high_i = low_i + boxes[:, 2:3]
    high_j = low_j + boxes[:, 3:4]
    inbox = (coarse_i >= low_i) & (coarse_i < high_i) & (coarse_j >= low_j) & (coarse_j < high_j)
    middle = (
        (coarse_i > low_i) & (coarse_i < high_i - 1) & (coarse_j > low_j) & (coarse_j < high_j - 1)
    )
    return (inbox, middle)


def spread_table():
    width = TILE * 3
    index = jnp.arange(width * width, dtype=jnp.int32)
    owner = index // width // 3 * TILE + index % width // 3
    return (jnp.arange(TILE * TILE, dtype=jnp.int32)[:, None] == owner[None, :]).astype(jnp.float32)


def to_flat_tiles(field):
    rows, cols = field.shape
    along_x = rows // TILE
    along_y = cols // TILE
    shaped = field.reshape(along_x, TILE, along_y, TILE).transpose(0, 2, 1, 3)
    return shaped.reshape(1, 1, along_x * along_y, TILE * TILE)


def from_tiles(tiles, block_rows, block_cols):
    along_x = block_rows // TILE
    along_y = block_cols // TILE
    shaped = tiles.reshape(along_x, along_y, TILE, TILE).transpose(0, 2, 1, 3)
    return shaped.reshape(block_rows, block_cols)


def pad_last(array, before, after):
    widths = [(0, 0)] * (array.ndim - 1) + [(before, after)]
    return jnp.pad(array, widths)


def fine_substep(fine_ez, fine_hx, fine_hy, damp, gain, inbox, middle, border, cycle_value):
    width = TILE * 3
    column = jnp.arange(width * width, dtype=jnp.int32) % width
    ez_next_col = jnp.where(column < width - 1, pad_last(fine_ez[..., 1:], 0, 1), 0.0)
    ez_next_row = pad_last(fine_ez[..., width:], 0, width)
    fine_hx = jnp.where(inbox, fine_hx - HCOEF * (ez_next_col - fine_ez), 0.0)
    fine_hy = jnp.where(inbox, fine_hy + HCOEF * (ez_next_row - fine_ez), 0.0)
    hy_prev = pad_last(fine_hy[..., :-width], width, 0)
    hx_prev = jnp.where(column > 0, pad_last(fine_hx[..., :-1], 1, 0), 0.0)
    curl = fine_hy - hy_prev - (fine_hx - hx_prev)
    inner = damp * fine_ez + gain * curl
    fine_ez = jnp.where(middle, inner, jnp.where(border, cycle_value, 0.0))
    return (fine_ez, fine_hx, fine_hy)


def fine_round(
    fine_ez, fine_hx, fine_hy, damp, gain, inbox, middle, border, old_tiles, new_tiles, spread
):
    for sub in range(1, 4):
        weight = sub / 3.0
        mixed = (1.0 - weight) * old_tiles + weight * new_tiles
        cycle_value = jnp.dot(
            mixed, spread, precision=lax.Precision.HIGHEST, preferred_element_type=jnp.float32
        )
        fine_ez, fine_hx, fine_hy = fine_substep(
            fine_ez, fine_hx, fine_hy, damp, gain, inbox, middle, border, cycle_value
        )
    return (fine_ez, fine_hx, fine_hy)


def coarse_magnetic(ez, hx, hy):
    below = passed_along(ez[:1, :], "gx", -1)
    beside = passed_along(ez[:, :1], ("grp", "gy"), -1)
    ez_next_row = jnp.concatenate([ez[1:, :], below], axis=0)
    ez_next_col = jnp.concatenate([ez[:, 1:], beside], axis=1)
    hx = hx - HCOEF * (ez_next_col - ez)
    hy = hy + HCOEF * (ez_next_row - ez)
    above = passed_along(hy[-1:, :], "gx", 1)
    before = passed_along(hx[:, -1:], ("grp", "gy"), 1)
    hy_prev = jnp.concatenate([above, hy[:-1, :]], axis=0)
    hx_prev = jnp.concatenate([before, hx[:, :-1]], axis=1)
    curl = hy - hy_prev - (hx - hx_prev)
    return (hx, hy, curl)


def shards(
    coarse_ez,
    coarse_hx,
    coarse_hy,
    coarse_ids,
    mat_eps,
    mat_sig,
    fine_ez,
    fine_hx,
    fine_hy,
    fine_ids,
    boxes,
    src_cells,
    src_wave,
    rcv_cells,
):
    rows, cols = coarse_ez.shape
    fine_shape = fine_ez.shape
    flat_cells = fine_shape[-1]
    means_shape = fine_shape[:-1] + (TILE * TILE,)
    row_start = lax.axis_index("gx") * rows
    col_start = lax.axis_index(("grp", "gy")) * cols
    all_cols = cols * lax.axis_size(("grp", "gy"))
    spread = spread_table()
    damp, gain = coefficients(coarse_ids, mat_eps, mat_sig, 1.0)
    fine_damp, fine_gain = coefficients(fine_ids.reshape(-1, flat_cells), mat_eps, mat_sig, 3.0)
    owned_boxes = lax.all_to_all(boxes, "gx", split_axis=2, concat_axis=0, tiled=True).reshape(
        -1, 4
    )
    inbox, middle = flat_masks(owned_boxes)
    border = inbox & jnp.logical_not(middle)
    coarse_mid = from_tiles(box_masks(boxes, TILE, 1)[1], rows, cols)
    src_rows = (
        jnp.arange(rows, dtype=jnp.int32)[None, :] == (src_cells // all_cols - row_start)[:, None]
    ).astype(jnp.float32)
    src_cols = (
        jnp.arange(cols, dtype=jnp.int32)[None, :] == (src_cells % all_cols - col_start)[:, None]
    ).astype(jnp.float32)
    rcv_rows = (
        jnp.arange(rows, dtype=jnp.int32)[None, :] == (rcv_cells // all_cols - row_start)[:, None]
    ).astype(jnp.float32)
    rcv_cols = (
        jnp.arange(cols, dtype=jnp.int32)[None, :] == (rcv_cells % all_cols - col_start)[:, None]
    ).astype(jnp.float32)
    ez, hx, hy = (coarse_ez, coarse_hx, coarse_hy)
    field_ez = fine_ez.reshape(-1, flat_cells)
    field_hx = fine_hx.reshape(-1, flat_cells)
    field_hy = fine_hy.reshape(-1, flat_cells)
    held = lax.all_to_all(to_flat_tiles(ez), "gx", split_axis=2, concat_axis=0, tiled=True).reshape(
        -1, TILE * TILE
    )
    samples = []
    for step in range(STEPS):
        hx, hy, curl = coarse_magnetic(ez, hx, hy)
        weighted = src_rows * src_wave[step][:, None]
        drive = jnp.dot(
            weighted.T,
            src_cols,
            precision=lax.Precision.HIGHEST,
            preferred_element_type=jnp.float32,
        )
        new = damp * ez + gain * curl + drive
        old_tiles = held
        new_tiles = lax.all_to_all(
            to_flat_tiles(new), "gx", split_axis=2, concat_axis=0, tiled=True
        ).reshape(-1, TILE * TILE)
        held = new_tiles
        field_ez, field_hx, field_hy = fine_round(
            field_ez,
            field_hx,
            field_hy,
            fine_damp,
            fine_gain,
            inbox,
            middle,
            border,
            old_tiles,
            new_tiles,
            spread,
        )
        sums = lax.dot_general(
            field_ez,
            spread,
            (((1,), (1,)), ((), ())),
            precision=lax.Precision.HIGHEST,
            preferred_element_type=jnp.float32,
        )
        means = (sums / 9.0).reshape(means_shape)
        back = lax.all_to_all(means, "gx", split_axis=0, concat_axis=2, tiled=True)
        ez = jnp.where(coarse_mid, from_tiles(back, rows, cols), new)
        picked = jnp.dot(
            rcv_rows, ez, precision=lax.Precision.HIGHEST, preferred_element_type=jnp.float32
        )
        samples.append(jnp.sum(picked * rcv_cols, axis=1))
    traces = lax.psum(jnp.stack(samples), ("grp", "gx", "gy"))
    return (
        ez,
        hx,
        hy,
        field_ez.reshape(fine_shape),
        field_hx.reshape(fine_shape),
        field_hy.reshape(fine_shape),
        traces,
    )


def solution(mesh):
    placed = (
        P("gx", ("grp", "gy")),
        P("gx", ("grp", "gy")),
        P("gx", ("grp", "gy")),
        P("gx", ("grp", "gy")),
        P(),
        P(),
        P(None, ("grp", "gy"), "gx", None),
        P(None, ("grp", "gy"), "gx", None),
        P(None, ("grp", "gy"), "gx", None),
        P(None, ("grp", "gy"), "gx", None),
        P("gx", ("grp", "gy"), None, None),
        P(),
        P(),
        P(),
    )
    return jax.shard_map(
        shards,
        mesh=mesh,
        in_specs=placed,
        out_specs=(
            P("gx", ("grp", "gy")),
            P("gx", ("grp", "gy")),
            P("gx", ("grp", "gy")),
            P(None, ("grp", "gy"), "gx", None),
            P(None, ("grp", "gy"), "gx", None),
            P(None, ("grp", "gy"), "gx", None),
            P(),
        ),
        check_vma=False,
    )
```

profile of v0, /device:TPU:0, one launch (start us, length us, event | category | flops | bytes accessed | tf_op | source)
XLA Modules:
  0.0 221.0 jit_solution(844649320013483524)
XLA Ops:
  0.7 1.4 copy.34
  2.1 6.3 %all-to-all-start = ((s32[1,1,32,4]{3,1,0,2:T(1,128)}), s32[1,1,32,4]{3,1,0,2:T(1,128)S(1)}, u32[]{:S(2)}, u32[]{:S(2)}) async-start(s32[1,1,32,4]{3,1,0,2:T(1,128)} %copy.34), calls=%async_computation | async-start | bytes 32768 | tf_op jit(solution)/shard_map/all_to_all | solution.py:158
  8.4 1.3 collective-permute-start.2
  10.4 1.3 collective-permute-start
  11.7 0.9 slice_reduce_fusion.1
  12.6 1.6 fusion.129
  14.2 1.6 fusion.128
  50.6 0.8 reshape.417
  51.5 4.6 %collective-permute-start.1 = (f32[1,128]{1,0:T(1,128)S(1)}, f32[1,128]{1,0:T(1,128)S(1)}, u32[]{:S(2)}, u32[]{:S(2)}) collective-permute-start(f32[1,128]{1,0:T(1,128)S(1)} %slice.384), channel_id=1, source_target_pairs={{0,4},{4,8},{8,12},{1,5},{5,9},{9,13},{2,6},{6,10},{10,14},{3,7},{... | collective-permute-start | bytes 1544 | tf_op jit(solution)/shard_map/ppermute | solution.py:15
  56.1 4.6 %collective-permute-start.3 = (f32[64,1]{1,0:T(8,128)S(1)}, f32[64,1]{1,0:T(8,128)S(1)}, u32[]{:S(2)}, u32[]{:S(2)}) collective-permute-start(f32[64,1]{1,0:T(8,128)S(1)} %slice.386), channel_id=1, source_target_pairs={{0,1},{1,2},{2,3},{3,16},{16,17},{17,18},{18,19},{4,5},{5,6},{6,7}... | collective-permute-start | bytes 776 | tf_op jit(solution)/shard_map/ppermute | solution.py:15
  60.7 4.2 %all-to-all-start.1 = ((f32[1,1,32,256]{3,1,0,2:T(1,128)}), f32[1,1,32,256]{3,1,0,2:T(1,128)S(1)}, u32[]{:S(2)}, u32[]{:S(2)}) async-start(f32[1,1,32,256]{3,1,0,2:T(1,128)} %reshape.417), calls=%async_computation.1 | async-start | bytes 65536 | tf_op jit(solution)/shard_map/all_to_all | solution.py:180
  66.3 4.3 %all-to-all-done.1 = f32[1,1,32,256]{3,1,0,2:T(1,128)S(1)} async-done(((f32[1,1,32,256]{3,1,0,2:T(1,128)}), f32[1,1,32,256]{3,1,0,2:T(1,128)S(1)}, u32[]{:S(2)}, u32[]{:S(2)}) %all-to-all-start.1) | async-done | bytes 32800 | tf_op jit(solution)/shard_map/all_to_all | solution.py:180
  70.5 3.3 %all-to-all-start.2 = ((f32[1,1,32,256]{3,1,0,2:T(1,128)}), f32[1,1,32,256]{3,1,0,2:T(1,128)S(1)}, u32[]{:S(2)}, u32[]{:S(2)}) async-start(f32[1,1,32,256]{3,1,0,2:T(1,128)} %reshape.418), calls=%async_computation.2 | async-start | bytes 65536 | tf_op jit(solution)/shard_map/all_to_all | solution.py:195
  74.1 5.3 %all-to-all-done.2 = f32[1,1,32,256]{3,1,0,2:T(1,128)S(1)} async-done(((f32[1,1,32,256]{3,1,0,2:T(1,128)}), f32[1,1,32,256]{3,1,0,2:T(1,128)S(1)}, u32[]{:S(2)}, u32[]{:S(2)}) %all-to-all-start.2) | async-done | bytes 32800 | tf_op jit(solution)/shard_map/all_to_all | solution.py:195
  79.5 1.0 fusion
  81.2 1.0 fusion.1
  82.8 1.0 fusion.2
  83.8 1.8 fusion.28
  85.6 3.3 %all-to-all-start.3 = ((f32[4,1,8,256]{3,2,1,0:T(8,128)}), f32[4,1,8,256]{3,2,1,0:T(8,128)S(1)}, u32[]{:S(2)}, u32[]{:S(2)}) async-start(f32[4,1,8,256]{3,2,1,0:T(8,128)} %fusion.28), calls=%async_computation.3 | async-start | bytes 65536 | tf_op jit(solution)/shard_map/all_to_all | solution.py:220
  89.2 5.3 %all-to-all-done.3 = f32[4,1,8,256]{3,2,1,0:T(8,128)S(1)} async-done(((f32[4,1,8,256]{3,2,1,0:T(8,128)}), f32[4,1,8,256]{3,2,1,0:T(8,128)S(1)}, u32[]{:S(2)}, u32[]{:S(2)}) %all-to-all-start.3) | async-done | bytes 32800 | tf_op jit(solution)/shard_map/all_to_all | solution.py:220
  94.9 1.3 collective-permute-start.4
  96.2 1.3 collective-permute-start.6
  97.6 4.8 %collective-permute-done.6 = f32[64,1]{1,0:T(8,128)S(1)} collective-permute-done((f32[64,1]{1,0:T(8,128)S(1)}, f32[64,1]{1,0:T(8,128)S(1)}, u32[]{:S(2)}, u32[]{:S(2)}) %collective-permute-start.6) | collective-permute-done | bytes 288 | tf_op jit(solution)/shard_map/ppermute | solution.py:15
  102.5 4.5 %collective-permute-start.5 = (f32[1,128]{1,0:T(1,128)S(1)}, f32[1,128]{1,0:T(1,128)S(1)}, u32[]{:S(2)}, u32[]{:S(2)}) collective-permute-start(f32[1,128]{1,0:T(1,128)S(1)} %slice.402), channel_id=1, source_target_pairs={{0,4},{4,8},{8,12},{1,5},{5,9},{9,13},{2,6},{6,10},{10,14},{3,7},{... | collective-permute-start | bytes 1544 | tf_op jit(solution)/shard_map/ppermute | solution.py:15
  107.1 4.8 %collective-permute-start.7 = (f32[64,1]{1,0:T(8,128)S(1)}, f32[64,1]{1,0:T(8,128)S(1)}, u32[]{:S(2)}, u32[]{:S(2)}) collective-permute-start(f32[64,1]{1,0:T(8,128)S(1)} %slice.406), channel_id=1, source_target_pairs={{0,1},{1,2},{2,3},{3,16},{16,17},{17,18},{18,19},{4,5},{5,6},{6,7}... | collective-permute-start | bytes 776 | tf_op jit(solution)/shard_map/ppermute | solution.py:15
  112.2 1.3 collective-permute-done.7
  114.8 3.4 %all-to-all-start.4 = ((f32[1,1,32,256]{3,1,0,2:T(1,128)}), f32[1,1,32,256]{3,1,0,2:T(1,128)S(1)}, u32[]{:S(2)}, u32[]{:S(2)}) async-start(f32[1,1,32,256]{3,1,0,2:T(1,128)} %reshape.419), calls=%async_computation.4 | async-start | bytes 65536 | tf_op jit(solution)/shard_map/all_to_all | solution.py:195
  118.5 5.2 %all-to-all-done.4 = f32[1,1,32,256]{3,1,0,2:T(1,128)S(1)} async-done(((f32[1,1,32,256]{3,1,0,2:T(1,128)}), f32[1,1,32,256]{3,1,0,2:T(1,128)S(1)}, u32[]{:S(2)}, u32[]{:S(2)}) %all-to-all-start.4) | async-done | bytes 32800 | tf_op jit(solution)/shard_map/all_to_all | solution.py:195
  123.8 1.0 fusion.3
  125.4 1.0 fusion.4
  127.0 1.0 fusion.5
  128.1 1.2 fusion.30
  129.3 8.0 %all_to_all.32 = f32[4,1,8,256]{3,2,1,0:T(8,128)S(1)} all-to-all(f32[4,1,8,256]{3,2,1,0:T(8,128)S(1)} %fusion.30), channel_id=1, replica_groups=mesh['grp'=2,'gx'=4,'gy'=4] {'gx'}, dimensions={0} | all-to-all | bytes 65536 | tf_op jit(solution)/shard_map/all_to_all | solution.py:220
  137.7 1.3 collective-permute-start.10
  139.0 1.3 collective-permute-start.8
  140.4 3.4 %collective-permute-done.10 = f32[64,1]{1,0:T(8,128)S(1)} collective-permute-done((f32[64,1]{1,0:T(8,128)S(1)}, f32[64,1]{1,0:T(8,128)S(1)}, u32[]{:S(2)}, u32[]{:S(2)}) %collective-permute-start.10) | collective-permute-done | bytes 288 | tf_op jit(solution)/shard_map/ppermute | solution.py:15
  144.6 2.6 %collective-permute-start.9 = (f32[1,128]{1,0:T(1,128)S(1)}, f32[1,128]{1,0:T(1,128)S(1)}, u32[]{:S(2)}, u32[]{:S(2)}) collective-permute-start(f32[1,128]{1,0:T(1,128)S(1)} %slice.422), channel_id=1, source_target_pairs={{0,4},{4,8},{8,12},{1,5},{5,9},{9,13},{2,6},{6,10},{10,14},{3,7},{... | collective-permute-start | bytes 1544 | tf_op jit(solution)/shard_map/ppermute | solution.py:15
  147.3 4.8 %collective-permute-start.11 = (f32[64,1]{1,0:T(8,128)S(1)}, f32[64,1]{1,0:T(8,128)S(1)}, u32[]{:S(2)}, u32[]{:S(2)}) collective-permute-start(f32[64,1]{1,0:T(8,128)S(1)} %slice.426), channel_id=1, source_target_pairs={{0,1},{1,2},{2,3},{3,16},{16,17},{17,18},{18,19},{4,5},{5,6},{6,7}... | collective-permute-start | bytes 776 | tf_op jit(solution)/shard_map/ppermute | solution.py:15
  152.7 1.0 collective-permute-done.11
  155.0 3.3 %all-to-all-start.6 = ((f32[1,1,32,256]{3,1,0,2:T(1,128)}), f32[1,1,32,256]{3,1,0,2:T(1,128)S(1)}, u32[]{:S(2)}, u32[]{:S(2)}) async-start(f32[1,1,32,256]{3,1,0,2:T(1,128)} %reshape.420), calls=%async_computation.6 | async-start | bytes 65536 | tf_op jit(solution)/shard_map/all_to_all | solution.py:195
  158.6 5.4 %all-to-all-done.6 = f32[1,1,32,256]{3,1,0,2:T(1,128)S(1)} async-done(((f32[1,1,32,256]{3,1,0,2:T(1,128)}), f32[1,1,32,256]{3,1,0,2:T(1,128)S(1)}, u32[]{:S(2)}, u32[]{:S(2)}) %all-to-all-start.6) | async-done | bytes 32800 | tf_op jit(solution)/shard_map/all_to_all | solution.py:195
  164.0 1.0 fusion.6
  165.6 1.0 fusion.7
  167.3 1.0 fusion.8
  168.3 1.8 fusion.32
  170.2 3.3 %all-to-all-start.7 = ((f32[4,1,8,256]{3,2,1,0:T(8,128)}), f32[4,1,8,256]{3,2,1,0:T(8,128)S(1)}, u32[]{:S(2)}, u32[]{:S(2)}) async-start(f32[4,1,8,256]{3,2,1,0:T(8,128)} %fusion.32), calls=%async_computation.7 | async-start | bytes 65536 | tf_op jit(solution)/shard_map/all_to_all | solution.py:220
  173.8 5.3 %all-to-all-done.7 = f32[4,1,8,256]{3,2,1,0:T(8,128)S(1)} async-done(((f32[4,1,8,256]{3,2,1,0:T(8,128)}), f32[4,1,8,256]{3,2,1,0:T(8,128)S(1)}, u32[]{:S(2)}, u32[]{:S(2)}) %all-to-all-start.7) | async-done | bytes 32800 | tf_op jit(solution)/shard_map/all_to_all | solution.py:220
  179.8 41.1 %psum.7 = f32[3,128]{1,0:T(4,128)} all-reduce(f32[3,128]{1,0:T(4,128)S(1)} %pad_maximum_fusion), channel_id=1, replica_groups=mesh['grp'=2,'gx'=4,'gy'=4] {'grp','gx','gy'}, use_global_device_ids=true, to_apply=%region_3.4 | all-reduce | flops 384 | bytes 3072 | tf_op jit(solution)/shard_map/psum | solution.py:226
  (142 shorter events, 16.6 us)
Async XLA Ops:
  0.6 46.8 %copy-start.13 = (f32[3,4]{1,0:T(4,128)S(1)}, f32[3,4]{1,0:T(4,128)}, u32[]{:S(2)}) copy-start(f32[3,4]{1,0:T(4,128)} %param.26) | copy-start | bytes 148
  0.6 46.9 %copy-start.14 = (s32[4]{0:T(128)S(1)}, s32[4]{0:T(128)}, u32[]{:S(2)}) copy-start(s32[4]{0:T(128)} %param.25) | copy-start | bytes 52
  0.7 47.0 %copy-start.4 = (s32[4,1,8,2304]{3,2,1,0:T(8,128)S(1)}, s32[4,1,8,2304]{3,2,1,0:T(8,128)}, u32[]{:S(2)}) copy-start(s32[4,1,8,2304]{3,2,1,0:T(8,128)} %param.23) | copy-start | bytes 884740
  2.1 58.6 %all-to-all-start = ((s32[1,1,32,4]{3,1,0,2:T(1,128)}), s32[1,1,32,4]{3,1,0,2:T(1,128)S(1)}, u32[]{:S(2)}, u32[]{:S(2)}) async-start(s32[1,1,32,4]{3,1,0,2:T(1,128)} %copy.34), calls=%async_computation | async-start | bytes 32768 | tf_op jit(solution)/shard_map/all_to_all | solution.py:158
  8.4 42.9 %collective-permute-start.2 = (f32[64,1]{1,0:T(8,128)}, f32[64,1]{1,0:T(8,128)S(1)}, u32[]{:S(2)}, u32[]{:S(2)}) collective-permute-start(f32[64,1]{1,0:T(8,128)} %bitcast.267), channel_id=1, source_target_pairs={{1,0},{2,1},{3,2},{16,3},{17,16},{18,17},{19,18},{5,4},{6,5},{7,6}... | collective-permute-start | bytes 776 | tf_op jit(solution)/shard_map/ppermute | solution.py:15
  10.4 41.0 %collective-permute-start = (f32[1,128]{1,0:T(1,128)S(1)}, f32[1,128]{1,0:T(1,128)S(1)}, u32[]{:S(2)}, u32[]{:S(2)}) collective-permute-start(f32[1,128]{1,0:T(1,128)S(1)} %slice.322), channel_id=1, source_target_pairs={{4,0},{8,4},{12,8},{5,1},{9,5},{13,9},{6,2},{10,6},{14,10},{7,3},{... | collective-permute-start | bytes 1544 | tf_op jit(solution)/shard_map/ppermute | solution.py:15
  47.6 0.8 copy-start.10
  48.4 1.0 copy-start
  49.5 0.8 copy-start.1
  50.5 0.9 copy-start.11
  50.5 0.8 copy-start.12
  51.5 13.5 %collective-permute-start.1 = (f32[1,128]{1,0:T(1,128)S(1)}, f32[1,128]{1,0:T(1,128)S(1)}, u32[]{:S(2)}, u32[]{:S(2)}) collective-permute-start(f32[1,128]{1,0:T(1,128)S(1)} %slice.384), channel_id=1, source_target_pairs={{0,4},{4,8},{8,12},{1,5},{5,9},{9,13},{2,6},{6,10},{10,14},{3,7},{... | collective-permute-start | bytes 1544 | tf_op jit(solution)/shard_map/ppermute | solution.py:15
  56.1 8.9 %collective-permute-start.3 = (f32[64,1]{1,0:T(8,128)S(1)}, f32[64,1]{1,0:T(8,128)S(1)}, u32[]{:S(2)}, u32[]{:S(2)}) collective-permute-start(f32[64,1]{1,0:T(8,128)S(1)} %slice.386), channel_id=1, source_target_pairs={{0,1},{1,2},{2,3},{3,16},{16,17},{17,18},{18,19},{4,5},{5,6},{6,7}... | collective-permute-start | bytes 776 | tf_op jit(solution)/shard_map/ppermute | solution.py:15
  60.7 9.9 %all-to-all-start.1 = ((f32[1,1,32,256]{3,1,0,2:T(1,128)}), f32[1,1,32,256]{3,1,0,2:T(1,128)S(1)}, u32[]{:S(2)}, u32[]{:S(2)}) async-start(f32[1,1,32,256]{3,1,0,2:T(1,128)} %reshape.417), calls=%async_computation.1 | async-start | bytes 65536 | tf_op jit(solution)/shard_map/all_to_all | solution.py:180
  65.4 8.4 %copy-start.6 = (f32[4,1,8,2304]{3,2,1,0:T(8,128)S(1)}, f32[4,1,8,2304]{3,2,1,0:T(8,128)}, u32[]{:S(2)}) copy-start(f32[4,1,8,2304]{3,2,1,0:T(8,128)} %param.21) | copy-start | bytes 884740
  65.5 8.3 %copy-start.5 = (f32[4,1,8,2304]{3,2,1,0:T(8,128)S(1)}, f32[4,1,8,2304]{3,2,1,0:T(8,128)}, u32[]{:S(2)}) copy-start(f32[4,1,8,2304]{3,2,1,0:T(8,128)} %param.22) | copy-start | bytes 884740
  70.5 8.9 %all-to-all-start.2 = ((f32[1,1,32,256]{3,1,0,2:T(1,128)}), f32[1,1,32,256]{3,1,0,2:T(1,128)S(1)}, u32[]{:S(2)}, u32[]{:S(2)}) async-start(f32[1,1,32,256]{3,1,0,2:T(1,128)} %reshape.418), calls=%async_computation.2 | async-start | bytes 65536 | tf_op jit(solution)/shard_map/all_to_all | solution.py:195
  85.6 8.9 %all-to-all-start.3 = ((f32[4,1,8,256]{3,2,1,0:T(8,128)}), f32[4,1,8,256]{3,2,1,0:T(8,128)S(1)}, u32[]{:S(2)}, u32[]{:S(2)}) async-start(f32[4,1,8,256]{3,2,1,0:T(8,128)} %fusion.28), calls=%async_computation.3 | async-start | bytes 65536 | tf_op jit(solution)/shard_map/all_to_all | solution.py:220
  94.9 7.5 %collective-permute-start.4 = (f32[1,128]{1,0:T(1,128)S(1)}, f32[1,128]{1,0:T(1,128)S(1)}, u32[]{:S(2)}, u32[]{:S(2)}) collective-permute-start(f32[1,128]{1,0:T(1,128)S(1)} %slice.401), channel_id=1, source_target_pairs={{4,0},{8,4},{12,8},{5,1},{9,5},{13,9},{6,2},{10,6},{14,10},{7,3},{... | collective-permute-start | bytes 1544 | tf_op jit(solution)/shard_map/ppermute | solution.py:15
  96.2 6.2 %collective-permute-start.6 = (f32[64,1]{1,0:T(8,128)S(1)}, f32[64,1]{1,0:T(8,128)S(1)}, u32[]{:S(2)}, u32[]{:S(2)}) collective-permute-start(f32[64,1]{1,0:T(8,128)S(1)} %bitcast.268), channel_id=1, source_target_pairs={{1,0},{2,1},{3,2},{16,3},{17,16},{18,17},{19,18},{5,4},{6,5},{7,6}... | collective-permute-start | bytes 776 | tf_op jit(solution)/shard_map/ppermute | solution.py:15
  102.5 11.0 %collective-permute-start.5 = (f32[1,128]{1,0:T(1,128)S(1)}, f32[1,128]{1,0:T(1,128)S(1)}, u32[]{:S(2)}, u32[]{:S(2)}) collective-permute-start(f32[1,128]{1,0:T(1,128)S(1)} %slice.402), channel_id=1, source_target_pairs={{0,4},{4,8},{8,12},{1,5},{5,9},{9,13},{2,6},{6,10},{10,14},{3,7},{... | collective-permute-start | bytes 1544 | tf_op jit(solution)/shard_map/ppermute | solution.py:15
  107.1 6.4 %collective-permute-start.7 = (f32[64,1]{1,0:T(8,128)S(1)}, f32[64,1]{1,0:T(8,128)S(1)}, u32[]{:S(2)}, u32[]{:S(2)}) collective-permute-start(f32[64,1]{1,0:T(8,128)S(1)} %slice.406), channel_id=1, source_target_pairs={{0,1},{1,2},{2,3},{3,16},{16,17},{17,18},{18,19},{4,5},{5,6},{6,7}... | collective-permute-start | bytes 776 | tf_op jit(solution)/shard_map/ppermute | solution.py:15
  114.8 8.9 %all-to-all-start.4 = ((f32[1,1,32,256]{3,1,0,2:T(1,128)}), f32[1,1,32,256]{3,1,0,2:T(1,128)S(1)}, u32[]{:S(2)}, u32[]{:S(2)}) async-start(f32[1,1,32,256]{3,1,0,2:T(1,128)} %reshape.419), calls=%async_computation.4 | async-start | bytes 65536 | tf_op jit(solution)/shard_map/all_to_all | solution.py:195
  137.5 2.8 %copy-start.15 = (s32[128]{0:T(128)S(1)}, s32[128]{0:T(128)}, u32[]{:S(2)}) copy-start(s32[128]{0:T(128)} %param.27) | copy-start | bytes 1540
  137.7 6.1 %collective-permute-start.10 = (f32[64,1]{1,0:T(8,128)S(1)}, f32[64,1]{1,0:T(8,128)S(1)}, u32[]{:S(2)}, u32[]{:S(2)}) collective-permute-start(f32[64,1]{1,0:T(8,128)S(1)} %bitcast.270), channel_id=1, source_target_pairs={{1,0},{2,1},{3,2},{16,3},{17,16},{18,17},{19,18},{5,4},{6,5},{7,6}... | collective-permute-start | bytes 776 | tf_op jit(solution)/shard_map/ppermute | solution.py:15
  139.0 5.5 %collective-permute-start.8 = (f32[1,128]{1,0:T(1,128)S(1)}, f32[1,128]{1,0:T(1,128)S(1)}, u32[]{:S(2)}, u32[]{:S(2)}) collective-permute-start(f32[1,128]{1,0:T(1,128)S(1)} %slice.421), channel_id=1, source_target_pairs={{4,0},{8,4},{12,8},{5,1},{9,5},{13,9},{6,2},{10,6},{14,10},{7,3},{... | collective-permute-start | bytes 1544 | tf_op jit(solution)/shard_map/ppermute | solution.py:15
  144.5 9.2 %copy-start.2 = (f32[64,128]{1,0:T(8,128)}, f32[64,128]{1,0:T(8,128)S(1)}, u32[]{:S(2)}) copy-start(f32[64,128]{1,0:T(8,128)S(1)} %get-tuple-element.77) | copy-start | bytes 98308
  144.5 9.2 %copy-start.3 = (f32[64,128]{1,0:T(8,128)}, f32[64,128]{1,0:T(8,128)S(1)}, u32[]{:S(2)}) copy-start(f32[64,128]{1,0:T(8,128)S(1)} %get-tuple-element.78) | copy-start | bytes 98308
  144.6 9.2 %collective-permute-start.9 = (f32[1,128]{1,0:T(1,128)S(1)}, f32[1,128]{1,0:T(1,128)S(1)}, u32[]{:S(2)}, u32[]{:S(2)}) collective-permute-start(f32[1,128]{1,0:T(1,128)S(1)} %slice.422), channel_id=1, source_target_pairs={{0,4},{4,8},{8,12},{1,5},{5,9},{9,13},{2,6},{6,10},{10,14},{3,7},{... | collective-permute-start | bytes 1544 | tf_op jit(solution)/shard_map/ppermute | solution.py:15
  147.3 6.4 %collective-permute-start.11 = (f32[64,1]{1,0:T(8,128)S(1)}, f32[64,1]{1,0:T(8,128)S(1)}, u32[]{:S(2)}, u32[]{:S(2)}) collective-permute-start(f32[64,1]{1,0:T(8,128)S(1)} %slice.426), channel_id=1, source_target_pairs={{0,1},{1,2},{2,3},{3,16},{16,17},{17,18},{18,19},{4,5},{5,6},{6,7}... | collective-permute-start | bytes 776 | tf_op jit(solution)/shard_map/ppermute | solution.py:15
  155.0 8.9 %all-to-all-start.6 = ((f32[1,1,32,256]{3,1,0,2:T(1,128)}), f32[1,1,32,256]{3,1,0,2:T(1,128)S(1)}, u32[]{:S(2)}, u32[]{:S(2)}) async-start(f32[1,1,32,256]{3,1,0,2:T(1,128)} %reshape.420), calls=%async_computation.6 | async-start | bytes 65536 | tf_op jit(solution)/shard_map/all_to_all | solution.py:195
  167.3 1.1 copy-start.7
  167.3 1.1 copy-start.8
  168.3 1.9 copy-start.16
  170.2 8.9 %all-to-all-start.7 = ((f32[4,1,8,256]{3,2,1,0:T(8,128)}), f32[4,1,8,256]{3,2,1,0:T(8,128)S(1)}, u32[]{:S(2)}, u32[]{:S(2)}) async-start(f32[4,1,8,256]{3,2,1,0:T(8,128)} %fusion.32), calls=%async_computation.7 | async-start | bytes 65536 | tf_op jit(solution)/shard_map/all_to_all | solution.py:220
  179.4 41.5 %copy-start.9 = (f32[64,128]{1,0:T(8,128)}, f32[64,128]{1,0:T(8,128)S(1)}, u32[]{:S(2)}) copy-start(f32[64,128]{1,0:T(8,128)S(1)} %select_n.630) | copy-start | bytes 98308
where the time goes:
time: 223 us; the launch traced here: 221 us
  starting transfers between devices  60.7 us (27%)
  blocking collectives  49.1 us (22%)
  waiting for transfers between devices  41.9 us (19%)
  between operations  32.9 us (15%)
  matrix products  15.9 us (7%)
  local copies, waits for them, and re-layouts  15.3 us (7%)
  other arithmetic  5.14 us (2%)
    psum x1, blocking collectives, shards(): traces = lax.psum(jnp.stack(samples), ('grp', 'gx', 'gy'))  41.1 us
    ppermute x12, starting transfers between devices, passed_along(): lax.ppermute(value, axis, [(source, source + steps) for source in range(i...  33.7 us
    all_to_all x3, waiting for transfers between devices, shards(): lax.all_to_all(to_flat_tiles(new), 'gx', split_axis=2, concat_axis=0, til...  15.8 us
    ppermute x12, waiting for transfers between devices, passed_along(): lax.ppermute(value, axis, [(source, source + steps) for source in range(i...  11.2 us
    all_to_all x2, waiting for transfers between devices, shards(): back = lax.all_to_all(means, 'gx', split_axis=0, concat_axis=2, tiled=True)  10.7 us
    all_to_all x3, starting transfers between devices, shards(): lax.all_to_all(to_flat_tiles(new), 'gx', split_axis=2, concat_axis=0, til...  9.97 us
    dot_general x9, matrix products, fine_round(): jnp.dot(mixed, spread, precision=lax.Precision.HIGHEST, preferred_element...  9.19 us
    all_to_all x1, blocking collectives, shards(): back = lax.all_to_all(means, 'gx', split_axis=0, concat_axis=2, tiled=True)  8.01 us
  transfers between devices with their start and end apart: 19, of which 11 were waited for; matrix products, arithmetic and copies ran while one was open for 5% of the time, Pallas kernels for 0%

commit v1 on v0

--- a/solution.py
+++ b/solution.py
@@ -1,3 +1,4 @@
+import functools
 import jax
 import jax.numpy as jnp
 from jax import lax
@@ -7,6 +8,14 @@
 STEPS = 3
 COURANT = 0.5
 HCOEF = 0.5
+
+
+def bars_detail(chunk, device_axis):
+    mid_arr = lax.all_gather(chunk, device_axis).sum(axis=0)
+    return mid_arr
+
+
+recover_the_samples_all = functools.partial(bars_detail, device_axis=("grp", "gx", "gy"))
 
 
 def passed_along(value, axis, steps):
@@ -223,7 +232,7 @@
             rcv_rows, ez, precision=lax.Precision.HIGHEST, preferred_element_type=jnp.float32
         )
         samples.append(jnp.sum(picked * rcv_cols, axis=1))
-    traces = lax.psum(jnp.stack(samples), ("grp", "gx", "gy"))
+    traces = recover_the_samples_all(jnp.stack(samples))
     return (
         ez,
         hx,

time: 223 us -> 249 us (1.12)
  blocking collectives: 49.1 us -> 74.6 us
    all_gather x0 -> x1, blocking collectives: none -> 66.6 us  [bars_detail(): mid_arr = lax.all_gather(chunk, device_axis).sum(axis=0)]
    psum x1 -> x0, blocking collectives: 41.1 us -> none  [shards(): traces = lax.psum(jnp.stack(samples), ('grp', 'gx', 'gy'))]
where the time goes in v1:
time: 249 us; the launch traced here: 247 us
  blocking collectives  74.6 us (30%)
  starting transfers between devices  60.7 us (24%)
  waiting for transfers between devices  41.9 us (17%)
  between operations  32.8 us (13%)
  matrix products  15.9 us (6%)
  local copies, waits for them, and re-layouts  15.3 us (6%)
  other arithmetic  5.76 us (2%)
    all_gather x1, blocking collectives, bars_detail(): mid_arr = lax.all_gather(chunk, device_axis).sum(axis=0)  66.6 us
    ppermute x12, starting transfers between devices, passed_along(): lax.ppermute(value, axis, [(source, source + steps) for source in range(i...  33.7 us
    all_to_all x3, waiting for transfers between devices, shards(): lax.all_to_all(to_flat_tiles(new), 'gx', split_axis=2, concat_axis=0, til...  15.8 us
    ppermute x12, waiting for transfers between devices, passed_along(): lax.ppermute(value, axis, [(source, source + steps) for source in range(i...  11.2 us
    all_to_all x2, waiting for transfers between devices, shards(): back = lax.all_to_all(means, 'gx', split_axis=0, concat_axis=2, tiled=True)  10.7 us
    all_to_all x3, starting transfers between devices, shards(): lax.all_to_all(to_flat_tiles(new), 'gx', split_axis=2, concat_axis=0, til...  9.97 us
    dot_general x9, matrix products, fine_round(): jnp.dot(mixed, spread, precision=lax.Precision.HIGHEST, preferred_element...  9.19 us
    all_to_all x1, blocking collectives, shards(): back = lax.all_to_all(means, 'gx', split_axis=0, concat_axis=2, tiled=True)  8.01 us
  transfers between devices with their start and end apart: 19, of which 11 were waited for; matrix products, arithmetic and copies ran while one was open for 5% of the time, Pallas kernels for 0%

profile of v1, /device:TPU:0, one launch (start us, length us, event | category | flops | bytes accessed | tf_op | source)
XLA Modules:
  0.0 247.0 jit_solution(6950932597651475403)
XLA Ops:
  0.7 1.4 copy.34
  2.1 6.3 %all-to-all-start = ((s32[1,1,32,4]{3,1,0,2:T(1,128)}), s32[1,1,32,4]{3,1,0,2:T(1,128)S(1)}, u32[]{:S(2)}, u32[]{:S(2)}) async-start(s32[1,1,32,4]{3,1,0,2:T(1,128)} %copy.34), calls=%async_computation | async-start | bytes 32768 | tf_op jit(solution)/shard_map/all_to_all | solution.py:167
  8.4 1.3 collective-permute-start.2
  10.4 1.3 collective-permute-start
  11.7 0.9 slice_reduce_fusion.1
  12.6 1.6 fusion.129
  14.2 1.6 fusion.128
  50.6 0.8 reshape.421
  51.5 4.6 %collective-permute-start.1 = (f32[1,128]{1,0:T(1,128)S(1)}, f32[1,128]{1,0:T(1,128)S(1)}, u32[]{:S(2)}, u32[]{:S(2)}) collective-permute-start(f32[1,128]{1,0:T(1,128)S(1)} %slice.384), channel_id=1, source_target_pairs={{0,4},{4,8},{8,12},{1,5},{5,9},{9,13},{2,6},{6,10},{10,14},{3,7},{... | collective-permute-start | bytes 1544 | tf_op jit(solution)/shard_map/ppermute | solution.py:24
  56.1 4.6 %collective-permute-start.3 = (f32[64,1]{1,0:T(8,128)S(1)}, f32[64,1]{1,0:T(8,128)S(1)}, u32[]{:S(2)}, u32[]{:S(2)}) collective-permute-start(f32[64,1]{1,0:T(8,128)S(1)} %slice.386), channel_id=1, source_target_pairs={{0,1},{1,2},{2,3},{3,16},{16,17},{17,18},{18,19},{4,5},{5,6},{6,7}... | collective-permute-start | bytes 776 | tf_op jit(solution)/shard_map/ppermute | solution.py:24
  60.7 4.2 %all-to-all-start.1 = ((f32[1,1,32,256]{3,1,0,2:T(1,128)}), f32[1,1,32,256]{3,1,0,2:T(1,128)S(1)}, u32[]{:S(2)}, u32[]{:S(2)}) async-start(f32[1,1,32,256]{3,1,0,2:T(1,128)} %reshape.421), calls=%async_computation.1 | async-start | bytes 65536 | tf_op jit(solution)/shard_map/all_to_all | solution.py:189
  66.3 4.3 %all-to-all-done.1 = f32[1,1,32,256]{3,1,0,2:T(1,128)S(1)} async-done(((f32[1,1,32,256]{3,1,0,2:T(1,128)}), f32[1,1,32,256]{3,1,0,2:T(1,128)S(1)}, u32[]{:S(2)}, u32[]{:S(2)}) %all-to-all-start.1) | async-done | bytes 32800 | tf_op jit(solution)/shard_map/all_to_all | solution.py:189
  70.5 3.3 %all-to-all-start.2 = ((f32[1,1,32,256]{3,1,0,2:T(1,128)}), f32[1,1,32,256]{3,1,0,2:T(1,128)S(1)}, u32[]{:S(2)}, u32[]{:S(2)}) async-start(f32[1,1,32,256]{3,1,0,2:T(1,128)} %reshape.422), calls=%async_computation.2 | async-start | bytes 65536 | tf_op jit(solution)/shard_map/all_to_all | solution.py:204
  74.1 5.3 %all-to-all-done.2 = f32[1,1,32,256]{3,1,0,2:T(1,128)S(1)} async-done(((f32[1,1,32,256]{3,1,0,2:T(1,128)}), f32[1,1,32,256]{3,1,0,2:T(1,128)S(1)}, u32[]{:S(2)}, u32[]{:S(2)}) %all-to-all-start.2) | async-done | bytes 32800 | tf_op jit(solution)/shard_map/all_to_all | solution.py:204
  79.5 1.0 fusion
  81.2 1.0 fusion.1
  82.8 1.0 fusion.2
  83.8 1.8 fusion.28
  85.6 3.3 %all-to-all-start.3 = ((f32[4,1,8,256]{3,2,1,0:T(8,128)}), f32[4,1,8,256]{3,2,1,0:T(8,128)S(1)}, u32[]{:S(2)}, u32[]{:S(2)}) async-start(f32[4,1,8,256]{3,2,1,0:T(8,128)} %fusion.28), calls=%async_computation.3 | async-start | bytes 65536 | tf_op jit(solution)/shard_map/all_to_all | solution.py:229
  89.2 5.3 %all-to-all-done.3 = f32[4,1,8,256]{3,2,1,0:T(8,128)S(1)} async-done(((f32[4,1,8,256]{3,2,1,0:T(8,128)}), f32[4,1,8,256]{3,2,1,0:T(8,128)S(1)}, u32[]{:S(2)}, u32[]{:S(2)}) %all-to-all-start.3) | async-done | bytes 32800 | tf_op jit(solution)/shard_map/all_to_all | solution.py:229
  94.9 1.3 collective-permute-start.4
  96.2 1.3 collective-permute-start.6
  97.6 4.8 %collective-permute-done.6 = f32[64,1]{1,0:T(8,128)S(1)} collective-permute-done((f32[64,1]{1,0:T(8,128)S(1)}, f32[64,1]{1,0:T(8,128)S(1)}, u32[]{:S(2)}, u32[]{:S(2)}) %collective-permute-start.6) | collective-permute-done | bytes 288 | tf_op jit(solution)/shard_map/ppermute | solution.py:24
  102.5 4.5 %collective-permute-start.5 = (f32[1,128]{1,0:T(1,128)S(1)}, f32[1,128]{1,0:T(1,128)S(1)}, u32[]{:S(2)}, u32[]{:S(2)}) collective-permute-start(f32[1,128]{1,0:T(1,128)S(1)} %slice.402), channel_id=1, source_target_pairs={{0,4},{4,8},{8,12},{1,5},{5,9},{9,13},{2,6},{6,10},{10,14},{3,7},{... | collective-permute-start | bytes 1544 | tf_op jit(solution)/shard_map/ppermute | solution.py:24
  107.1 4.8 %collective-permute-start.7 = (f32[64,1]{1,0:T(8,128)S(1)}, f32[64,1]{1,0:T(8,128)S(1)}, u32[]{:S(2)}, u32[]{:S(2)}) collective-permute-start(f32[64,1]{1,0:T(8,128)S(1)} %slice.406), channel_id=1, source_target_pairs={{0,1},{1,2},{2,3},{3,16},{16,17},{17,18},{18,19},{4,5},{5,6},{6,7}... | collective-permute-start | bytes 776 | tf_op jit(solution)/shard_map/ppermute | solution.py:24
  112.2 1.3 collective-permute-done.7
  114.8 3.4 %all-to-all-start.4 = ((f32[1,1,32,256]{3,1,0,2:T(1,128)}), f32[1,1,32,256]{3,1,0,2:T(1,128)S(1)}, u32[]{:S(2)}, u32[]{:S(2)}) async-start(f32[1,1,32,256]{3,1,0,2:T(1,128)} %reshape.423), calls=%async_computation.4 | async-start | bytes 65536 | tf_op jit(solution)/shard_map/all_to_all | solution.py:204
  118.5 5.2 %all-to-all-done.4 = f32[1,1,32,256]{3,1,0,2:T(1,128)S(1)} async-done(((f32[1,1,32,256]{3,1,0,2:T(1,128)}), f32[1,1,32,256]{3,1,0,2:T(1,128)S(1)}, u32[]{:S(2)}, u32[]{:S(2)}) %all-to-all-start.4) | async-done | bytes 32800 | tf_op jit(solution)/shard_map/all_to_all | solution.py:204
  123.8 1.0 fusion.3
  125.4 1.0 fusion.4
  127.0 1.0 fusion.5
  128.1 1.2 fusion.30
  129.3 8.0 %all_to_all.32 = f32[4,1,8,256]{3,2,1,0:T(8,128)S(1)} all-to-all(f32[4,1,8,256]{3,2,1,0:T(8,128)S(1)} %fusion.30), channel_id=1, replica_groups=mesh['grp'=2,'gx'=4,'gy'=4] {'gx'}, dimensions={0} | all-to-all | bytes 65536 | tf_op jit(solution)/shard_map/all_to_all | solution.py:229
  137.7 1.3 collective-permute-start.10
  139.0 1.3 collective-permute-start.8
  140.4 3.4 %collective-permute-done.10 = f32[64,1]{1,0:T(8,128)S(1)} collective-permute-done((f32[64,1]{1,0:T(8,128)S(1)}, f32[64,1]{1,0:T(8,128)S(1)}, u32[]{:S(2)}, u32[]{:S(2)}) %collective-permute-start.10) | collective-permute-done | bytes 288 | tf_op jit(solution)/shard_map/ppermute | solution.py:24
  144.6 2.6 %collective-permute-start.9 = (f32[1,128]{1,0:T(1,128)S(1)}, f32[1,128]{1,0:T(1,128)S(1)}, u32[]{:S(2)}, u32[]{:S(2)}) collective-permute-start(f32[1,128]{1,0:T(1,128)S(1)} %slice.422), channel_id=1, source_target_pairs={{0,4},{4,8},{8,12},{1,5},{5,9},{9,13},{2,6},{6,10},{10,14},{3,7},{... | collective-permute-start | bytes 1544 | tf_op jit(solution)/shard_map/ppermute | solution.py:24
  147.3 4.8 %collective-permute-start.11 = (f32[64,1]{1,0:T(8,128)S(1)}, f32[64,1]{1,0:T(8,128)S(1)}, u32[]{:S(2)}, u32[]{:S(2)}) collective-permute-start(f32[64,1]{1,0:T(8,128)S(1)} %slice.426), channel_id=1, source_target_pairs={{0,1},{1,2},{2,3},{3,16},{16,17},{17,18},{18,19},{4,5},{5,6},{6,7}... | collective-permute-start | bytes 776 | tf_op jit(solution)/shard_map/ppermute | solution.py:24
  152.7 1.0 collective-permute-done.11
  155.0 3.3 %all-to-all-start.6 = ((f32[1,1,32,256]{3,1,0,2:T(1,128)}), f32[1,1,32,256]{3,1,0,2:T(1,128)S(1)}, u32[]{:S(2)}, u32[]{:S(2)}) async-start(f32[1,1,32,256]{3,1,0,2:T(1,128)} %reshape.424), calls=%async_computation.6 | async-start | bytes 65536 | tf_op jit(solution)/shard_map/all_to_all | solution.py:204
  158.6 5.4 %all-to-all-done.6 = f32[1,1,32,256]{3,1,0,2:T(1,128)S(1)} async-done(((f32[1,1,32,256]{3,1,0,2:T(1,128)}), f32[1,1,32,256]{3,1,0,2:T(1,128)S(1)}, u32[]{:S(2)}, u32[]{:S(2)}) %all-to-all-start.6) | async-done | bytes 32800 | tf_op jit(solution)/shard_map/all_to_all | solution.py:204
  164.0 1.0 fusion.6
  165.6 1.0 fusion.7
  167.3 1.0 fusion.8
  168.3 1.8 fusion.32
  170.2 3.3 %all-to-all-start.7 = ((f32[4,1,8,256]{3,2,1,0:T(8,128)}), f32[4,1,8,256]{3,2,1,0:T(8,128)S(1)}, u32[]{:S(2)}, u32[]{:S(2)}) async-start(f32[4,1,8,256]{3,2,1,0:T(8,128)} %fusion.32), calls=%async_computation.7 | async-start | bytes 65536 | tf_op jit(solution)/shard_map/all_to_all | solution.py:229
  173.8 5.3 %all-to-all-done.7 = f32[4,1,8,256]{3,2,1,0:T(8,128)S(1)} async-done(((f32[4,1,8,256]{3,2,1,0:T(8,128)}), f32[4,1,8,256]{3,2,1,0:T(8,128)S(1)}, u32[]{:S(2)}, u32[]{:S(2)}) %all-to-all-start.7) | async-done | bytes 32800 | tf_op jit(solution)/shard_map/all_to_all | solution.py:229
  179.8 66.6 %all-gather.1 = f32[32,3,128]{2,1,0:T(4,128)S(1)} all-gather(f32[1,3,128]{2,1,0:T(4,128)S(1)} %maximum_bitcast_fusion), channel_id=2, replica_groups=mesh['grp'=2,'gx'=4,'gy'=4] {'grp','gx','gy'}, dimensions={0}, use_global_device_ids=true | all-gather | bytes 50688 | tf_op jit(solution)/shard_map/all_gather | solution.py:14
  (143 shorter events, 17.2 us)
Async XLA Ops:
  0.6 46.8 %copy-start.13 = (f32[3,4]{1,0:T(4,128)S(1)}, f32[3,4]{1,0:T(4,128)}, u32[]{:S(2)}) copy-start(f32[3,4]{1,0:T(4,128)} %param.26) | copy-start | bytes 148
  0.6 46.9 %copy-start.14 = (s32[4]{0:T(128)S(1)}, s32[4]{0:T(128)}, u32[]{:S(2)}) copy-start(s32[4]{0:T(128)} %param.25) | copy-start | bytes 52
  0.7 47.0 %copy-start.4 = (s32[4,1,8,2304]{3,2,1,0:T(8,128)S(1)}, s32[4,1,8,2304]{3,2,1,0:T(8,128)}, u32[]{:S(2)}) copy-start(s32[4,1,8,2304]{3,2,1,0:T(8,128)} %param.23) | copy-start | bytes 884740
  2.1 58.6 %all-to-all-start = ((s32[1,1,32,4]{3,1,0,2:T(1,128)}), s32[1,1,32,4]{3,1,0,2:T(1,128)S(1)}, u32[]{:S(2)}, u32[]{:S(2)}) async-start(s32[1,1,32,4]{3,1,0,2:T(1,128)} %copy.34), calls=%async_computation | async-start | bytes 32768 | tf_op jit(solution)/shard_map/all_to_all | solution.py:167
  8.4 42.9 %collective-permute-start.2 = (f32[64,1]{1,0:T(8,128)}, f32[64,1]{1,0:T(8,128)S(1)}, u32[]{:S(2)}, u32[]{:S(2)}) collective-permute-start(f32[64,1]{1,0:T(8,128)} %bitcast.269), channel_id=1, source_target_pairs={{1,0},{2,1},{3,2},{16,3},{17,16},{18,17},{19,18},{5,4},{6,5},{7,6}... | collective-permute-start | bytes 776 | tf_op jit(solution)/shard_map/ppermute | solution.py:24
  10.4 41.0 %collective-permute-start = (f32[1,128]{1,0:T(1,128)S(1)}, f32[1,128]{1,0:T(1,128)S(1)}, u32[]{:S(2)}, u32[]{:S(2)}) collective-permute-start(f32[1,128]{1,0:T(1,128)S(1)} %slice.322), channel_id=1, source_target_pairs={{4,0},{8,4},{12,8},{5,1},{9,5},{13,9},{6,2},{10,6},{14,10},{7,3},{... | collective-permute-start | bytes 1544 | tf_op jit(solution)/shard_map/ppermute | solution.py:24
  47.6 0.8 copy-start.10
  48.4 1.0 copy-start
  49.5 0.8 copy-start.1
  50.5 0.9 copy-start.11
  50.5 0.8 copy-start.12
  51.5 13.5 %collective-permute-start.1 = (f32[1,128]{1,0:T(1,128)S(1)}, f32[1,128]{1,0:T(1,128)S(1)}, u32[]{:S(2)}, u32[]{:S(2)}) collective-permute-start(f32[1,128]{1,0:T(1,128)S(1)} %slice.384), channel_id=1, source_target_pairs={{0,4},{4,8},{8,12},{1,5},{5,9},{9,13},{2,6},{6,10},{10,14},{3,7},{... | collective-permute-start | bytes 1544 | tf_op jit(solution)/shard_map/ppermute | solution.py:24
  56.1 8.9 %collective-permute-start.3 = (f32[64,1]{1,0:T(8,128)S(1)}, f32[64,1]{1,0:T(8,128)S(1)}, u32[]{:S(2)}, u32[]{:S(2)}) collective-permute-start(f32[64,1]{1,0:T(8,128)S(1)} %slice.386), channel_id=1, source_target_pairs={{0,1},{1,2},{2,3},{3,16},{16,17},{17,18},{18,19},{4,5},{5,6},{6,7}... | collective-permute-start | bytes 776 | tf_op jit(solution)/shard_map/ppermute | solution.py:24
  60.7 9.9 %all-to-all-start.1 = ((f32[1,1,32,256]{3,1,0,2:T(1,128)}), f32[1,1,32,256]{3,1,0,2:T(1,128)S(1)}, u32[]{:S(2)}, u32[]{:S(2)}) async-start(f32[1,1,32,256]{3,1,0,2:T(1,128)} %reshape.421), calls=%async_computation.1 | async-start | bytes 65536 | tf_op jit(solution)/shard_map/all_to_all | solution.py:189
  65.4 8.4 %copy-start.6 = (f32[4,1,8,2304]{3,2,1,0:T(8,128)S(1)}, f32[4,1,8,2304]{3,2,1,0:T(8,128)}, u32[]{:S(2)}) copy-start(f32[4,1,8,2304]{3,2,1,0:T(8,128)} %param.21) | copy-start | bytes 884740
  65.5 8.3 %copy-start.5 = (f32[4,1,8,2304]{3,2,1,0:T(8,128)S(1)}, f32[4,1,8,2304]{3,2,1,0:T(8,128)}, u32[]{:S(2)}) copy-start(f32[4,1,8,2304]{3,2,1,0:T(8,128)} %param.22) | copy-start | bytes 884740
  70.5 8.9 %all-to-all-start.2 = ((f32[1,1,32,256]{3,1,0,2:T(1,128)}), f32[1,1,32,256]{3,1,0,2:T(1,128)S(1)}, u32[]{:S(2)}, u32[]{:S(2)}) async-start(f32[1,1,32,256]{3,1,0,2:T(1,128)} %reshape.422), calls=%async_computation.2 | async-start | bytes 65536 | tf_op jit(solution)/shard_map/all_to_all | solution.py:204
  85.6 8.9 %all-to-all-start.3 = ((f32[4,1,8,256]{3,2,1,0:T(8,128)}), f32[4,1,8,256]{3,2,1,0:T(8,128)S(1)}, u32[]{:S(2)}, u32[]{:S(2)}) async-start(f32[4,1,8,256]{3,2,1,0:T(8,128)} %fusion.28), calls=%async_computation.3 | async-start | bytes 65536 | tf_op jit(solution)/shard_map/all_to_all | solution.py:229
  94.9 7.5 %collective-permute-start.4 = (f32[1,128]{1,0:T(1,128)S(1)}, f32[1,128]{1,0:T(1,128)S(1)}, u32[]{:S(2)}, u32[]{:S(2)}) collective-permute-start(f32[1,128]{1,0:T(1,128)S(1)} %slice.401), channel_id=1, source_target_pairs={{4,0},{8,4},{12,8},{5,1},{9,5},{13,9},{6,2},{10,6},{14,10},{7,3},{... | collective-permute-start | bytes 1544 | tf_op jit(solution)/shard_map/ppermute | solution.py:24
  96.2 6.2 %collective-permute-start.6 = (f32[64,1]{1,0:T(8,128)S(1)}, f32[64,1]{1,0:T(8,128)S(1)}, u32[]{:S(2)}, u32[]{:S(2)}) collective-permute-start(f32[64,1]{1,0:T(8,128)S(1)} %bitcast.270), channel_id=1, source_target_pairs={{1,0},{2,1},{3,2},{16,3},{17,16},{18,17},{19,18},{5,4},{6,5},{7,6}... | collective-permute-start | bytes 776 | tf_op jit(solution)/shard_map/ppermute | solution.py:24
  102.5 11.0 %collective-permute-start.5 = (f32[1,128]{1,0:T(1,128)S(1)}, f32[1,128]{1,0:T(1,128)S(1)}, u32[]{:S(2)}, u32[]{:S(2)}) collective-permute-start(f32[1,128]{1,0:T(1,128)S(1)} %slice.402), channel_id=1, source_target_pairs={{0,4},{4,8},{8,12},{1,5},{5,9},{9,13},{2,6},{6,10},{10,14},{3,7},{... | collective-permute-start | bytes 1544 | tf_op jit(solution)/shard_map/ppermute | solution.py:24
  107.1 6.4 %collective-permute-start.7 = (f32[64,1]{1,0:T(8,128)S(1)}, f32[64,1]{1,0:T(8,128)S(1)}, u32[]{:S(2)}, u32[]{:S(2)}) collective-permute-start(f32[64,1]{1,0:T(8,128)S(1)} %slice.406), channel_id=1, source_target_pairs={{0,1},{1,2},{2,3},{3,16},{16,17},{17,18},{18,19},{4,5},{5,6},{6,7}... | collective-permute-start | bytes 776 | tf_op jit(solution)/shard_map/ppermute | solution.py:24
  114.8 8.9 %all-to-all-start.4 = ((f32[1,1,32,256]{3,1,0,2:T(1,128)}), f32[1,1,32,256]{3,1,0,2:T(1,128)S(1)}, u32[]{:S(2)}, u32[]{:S(2)}) async-start(f32[1,1,32,256]{3,1,0,2:T(1,128)} %reshape.423), calls=%async_computation.4 | async-start | bytes 65536 | tf_op jit(solution)/shard_map/all_to_all | solution.py:204
  137.5 2.8 %copy-start.15 = (s32[128]{0:T(128)S(1)}, s32[128]{0:T(128)}, u32[]{:S(2)}) copy-start(s32[128]{0:T(128)} %param.27) | copy-start | bytes 1540
  137.7 6.1 %collective-permute-start.10 = (f32[64,1]{1,0:T(8,128)S(1)}, f32[64,1]{1,0:T(8,128)S(1)}, u32[]{:S(2)}, u32[]{:S(2)}) collective-permute-start(f32[64,1]{1,0:T(8,128)S(1)} %bitcast.272), channel_id=1, source_target_pairs={{1,0},{2,1},{3,2},{16,3},{17,16},{18,17},{19,18},{5,4},{6,5},{7,6}... | collective-permute-start | bytes 776 | tf_op jit(solution)/shard_map/ppermute | solution.py:24
  139.0 5.5 %collective-permute-start.8 = (f32[1,128]{1,0:T(1,128)S(1)}, f32[1,128]{1,0:T(1,128)S(1)}, u32[]{:S(2)}, u32[]{:S(2)}) collective-permute-start(f32[1,128]{1,0:T(1,128)S(1)} %slice.421), channel_id=1, source_target_pairs={{4,0},{8,4},{12,8},{5,1},{9,5},{13,9},{6,2},{10,6},{14,10},{7,3},{... | collective-permute-start | bytes 1544 | tf_op jit(solution)/shard_map/ppermute | solution.py:24
  144.5 9.2 %copy-start.2 = (f32[64,128]{1,0:T(8,128)}, f32[64,128]{1,0:T(8,128)S(1)}, u32[]{:S(2)}) copy-start(f32[64,128]{1,0:T(8,128)S(1)} %get-tuple-element.77) | copy-start | bytes 98308
  144.5 9.2 %copy-start.3 = (f32[64,128]{1,0:T(8,128)}, f32[64,128]{1,0:T(8,128)S(1)}, u32[]{:S(2)}) copy-start(f32[64,128]{1,0:T(8,128)S(1)} %get-tuple-element.78) | copy-start | bytes 98308
  144.6 9.2 %collective-permute-start.9 = (f32[1,128]{1,0:T(1,128)S(1)}, f32[1,128]{1,0:T(1,128)S(1)}, u32[]{:S(2)}, u32[]{:S(2)}) collective-permute-start(f32[1,128]{1,0:T(1,128)S(1)} %slice.422), channel_id=1, source_target_pairs={{0,4},{4,8},{8,12},{1,5},{5,9},{9,13},{2,6},{6,10},{10,14},{3,7},{... | collective-permute-start | bytes 1544 | tf_op jit(solution)/shard_map/ppermute | solution.py:24
  147.3 6.4 %collective-permute-start.11 = (f32[64,1]{1,0:T(8,128)S(1)}, f32[64,1]{1,0:T(8,128)S(1)}, u32[]{:S(2)}, u32[]{:S(2)}) collective-permute-start(f32[64,1]{1,0:T(8,128)S(1)} %slice.426), channel_id=1, source_target_pairs={{0,1},{1,2},{2,3},{3,16},{16,17},{17,18},{18,19},{4,5},{5,6},{6,7}... | collective-permute-start | bytes 776 | tf_op jit(solution)/shard_map/ppermute | solution.py:24
  155.0 8.9 %all-to-all-start.6 = ((f32[1,1,32,256]{3,1,0,2:T(1,128)}), f32[1,1,32,256]{3,1,0,2:T(1,128)S(1)}, u32[]{:S(2)}, u32[]{:S(2)}) async-start(f32[1,1,32,256]{3,1,0,2:T(1,128)} %reshape.424), calls=%async_computation.6 | async-start | bytes 65536 | tf_op jit(solution)/shard_map/all_to_all | solution.py:204
  167.3 1.1 copy-start.7
  167.3 1.1 copy-start.8
  168.3 1.9 copy-start.16
  170.2 8.9 %all-to-all-start.7 = ((f32[4,1,8,256]{3,2,1,0:T(8,128)}), f32[4,1,8,256]{3,2,1,0:T(8,128)S(1)}, u32[]{:S(2)}, u32[]{:S(2)}) async-start(f32[4,1,8,256]{3,2,1,0:T(8,128)} %fusion.32), calls=%async_computation.7 | async-start | bytes 65536 | tf_op jit(solution)/shard_map/all_to_all | solution.py:229
  179.4 67.6 %copy-start.9 = (f32[64,128]{1,0:T(8,128)}, f32[64,128]{1,0:T(8,128)S(1)}, u32[]{:S(2)}) copy-start(f32[64,128]{1,0:T(8,128)S(1)} %select_n.630) | copy-start | bytes 98308
